TPU v7x, 32 devices: a whole 2x2x4 slice. The times are simulated.
32 devices in a mesh: row: 8 (over y, x, core), col: 4 (over z).
Axes of the slice: x: 2, y: 2, z: 4, core: 2. Of those that a mesh axis runs over, the one named last changes fastest.
Arguments:
- a_window: float32 [16384, 4096], P('row', 'col'), may hold values from -6 to 6
- l_panel: float32 [16384, 1024], P('row'), may hold values from -0.1875 to 0.1875
- l_inverse: float32 [2, 512, 512], replicated, may hold values from -2 to 2, as said below
Outputs:
- reduced: float32 [16384, 4096], P('row', 'col')
Inputs may be any that keep to these rules, and one draw needn't show every extreme that they name: `l_inverse`: both blocks are lower triangular, with diagonal entries between 0.5 and 2.
All inputs are finite; a program needn't handle non-finite values.
Results may differ from a plain program's by a relative error of at most 0.000067.
Values sent between devices are 32-bit elements; how exact they have to be, the bound alone decides.
A program may use at most 128 MiB of HBM per device.

v0:
```python
import jax
import jax.numpy as jnp
from jax import lax
from jax.sharding import PartitionSpec as P


def spread(block, axis, holder):
    block = jnp.where(lax.axis_index(axis) == holder, block, jnp.zeros_like(block))
    return lax.psum(block, axis)


def matmul_hp(left, right):
    return jnp.dot(left, right, precision=lax.Precision.HIGHEST, preferred_element_type=jnp.float32)


def matmul_bt(left, right):
    return lax.dot_general(
        left,
        right,
        (((1,), (1,)), ((), ())),
        precision=lax.Precision.HIGHEST,
        preferred_element_type=jnp.float32,
    )


def body(a_window, l_panel, l_inverse):
    rows_dev = a_window.shape[0]
    half_size = l_inverse.shape[1]
    panel_width = a_window.shape[1]
    row_at = lax.axis_index("row")
    col_at = lax.axis_index("col")
    first_inv = l_inverse[0]
    second_inv = l_inverse[1]
    col_start = col_at * panel_width
    col_root = col_start // rows_dev
    col_offset = col_start % rows_dev
    row_block = spread(l_panel, "row", col_root)
    lower_col = lax.dynamic_slice_in_dim(row_block, col_offset, panel_width, 0)
    coupling = lower_col[half_size:panel_width, :half_size]
    panel_col = col_at == 0
    global_rows = row_at * rows_dev + lax.iota(jnp.int32, rows_dev)
    is_top = (global_rows < panel_width)[:, None]
    zeros_wide = jnp.zeros((rows_dev, panel_width), jnp.float32)
    zeros_block = jnp.zeros((panel_width, panel_width), jnp.float32)

    def solve_panel():
        leading = matmul_bt(a_window[:, :half_size], first_inv)
        second = matmul_bt(a_window[:, half_size:] - matmul_bt(leading, coupling), second_inv)
        return jnp.concatenate([leading, second], 1)

    solved = lax.cond(panel_col, solve_panel, lambda: zeros_wide)

    def block_solve(top_rows):
        upper_tile = matmul_hp(first_inv, top_rows[:half_size])
        lower_tile = matmul_hp(
            second_inv,
            top_rows[half_size:]
            - matmul_hp(l_panel[half_size:panel_width, :half_size], upper_tile),
        )
        return jnp.concatenate([upper_tile, lower_tile], 0)

    diag_part = lax.cond(
        jnp.logical_and(panel_col, row_at == 0),
        lambda: block_solve(solved[:panel_width]),
        lambda: zeros_block,
    )
    diag_block = spread(diag_part, "row", 0)

    def panel_math():
        product = matmul_hp(l_panel, diag_block)
        top_fill = jnp.pad(diag_block, ((0, rows_dev - panel_width), (0, 0)))
        result = jnp.where(is_top, top_fill, solved - product)
        return (result, solved - 0.5 * product)

    panel_out, g_part = lax.cond(panel_col, panel_math, lambda: (zeros_wide, zeros_wide))
    g_rows = spread(g_part, "col", 0)
    g_block = spread(g_rows, "row", col_root)
    g_col = lax.dynamic_slice_in_dim(g_block, col_offset, panel_width, 0)

    def trail_math():
        update = a_window - matmul_bt(l_panel, g_col) - matmul_bt(g_rows, lower_col)
        return jnp.where(is_top, a_window, update)

    return lax.cond(panel_col, lambda: panel_out, trail_math)


def solution(mesh):
    placed = (P("row", "col"), P("row", None), P())
    return jax.shard_map(
        body, mesh=mesh, in_specs=placed, out_specs=P("row", "col"), check_vma=False
    )
```

profile of v0, /device:TPU:27, one launch (start us, length us, event | category | flops | bytes accessed | tf_op | source)
XLA Modules:
  0.0 852.9 jit_solution(11067497493396346703)
XLA Ops:
  6.5 0.0 all-reduce.6.cloned.1.call-start
  6.5 5.3 broadcast_select_fusion.2
  11.8 0.0 all-reduce.6.cloned.1.call-update
  11.9 0.0 all-reduce.8.cloned.1.call-start
  11.9 1.7 slice_bitcast_fusion
  13.7 126.2 %all-reduce.6.cloned.1.call-done = f32[2048,1024]{1,0:T(8,128)} async-done(((f32[2048,1024]{1,0:T(8,128)}), f32[2048,1024]{1,0:T(8,128)}) %all-reduce.6.cloned.1.call-update) | async-done | bytes 8388624 | tf_op jit(solution)/shard_map/psum | solution.py:9
  139.9 4.8 constant_dynamic-slice_fusion
  144.7 13.2 %conditional.4 = (f32[2048,1024]{0,1:T(8,128)}) conditional(s32[]{:T(128)} %convert_element_type.10, () %tuple.37, (f32[2048,1024]{1,0:T(8,128)}, f32[512,512]{1,0:T(8,128)S(1)}, f32[1024,1024]{1,0:T(8,128)}, f32[512,512]{1,0:T(8,128)S(1)}) %tuple.38), branch_computations={%region_1.2_spmd, %region_2.3_spmd} | conditional | flops 19330498560 | bytes 74448952 | solution.py:51
  144.7 4.3 broadcast.28
  157.9 2.6 conditional.5
  157.9 2.5 broadcast.29
  160.5 2.8 broadcast_select_fusion.3
  163.3 0.0 all-reduce.8.cloned.1.call-update
  163.4 0.0 all-reduce.10.cloned.1.call-start
  163.4 125.2 %all-reduce.8.cloned.1.call-done = f32[1024,1024]{1,0:T(8,128)} async-done(((f32[1024,1024]{1,0:T(8,128)}), f32[1024,1024]{1,0:T(8,128)}) %all-reduce.8.cloned.1.call-update) | async-done | bytes 4194320 | tf_op jit(solution)/shard_map/psum | solution.py:9
  288.6 9.0 %conditional.6 = (f32[2048,1024]{1,0:T(8,128)}, f32[2048,1024]{1,0:T(8,128)}) conditional(s32[]{:T(128)} %convert_element_type.10, () %tuple.35, (f32[2048,1024]{1,0:T(8,128)}, f32[1024,1024]{1,0:T(8,128)}, f32[2048,1024]{0,1:T(8,128)}, pred[2048,1]{0,1:T(4,128)(4,1)S(1)}) %tuple.40), branch_computations={%region_6.7_spmd, %region_7.8_spmd} | conditional | flops 25778192384 | bytes 54532112 | solution.py:75
  288.6 4.5 broadcast.30.clone
  293.1 4.3 broadcast.30
  297.6 5.2 broadcast_select_fusion.1
  302.8 0.0 all-reduce.10.cloned.1.call-update
  302.8 0.0 all-reduce.12.cloned.1.call-start
  302.8 326.5 %all-reduce.10.cloned.1.call-done = f32[2048,1024]{1,0:T(8,128)} async-done(((f32[2048,1024]{1,0:T(8,128)}), f32[2048,1024]{1,0:T(8,128)}) %all-reduce.10.cloned.1.call-update) | async-done | bytes 8388624 | tf_op jit(solution)/shard_map/psum | solution.py:9
  629.3 5.1 broadcast_select_fusion
  634.5 0.0 all-reduce.12.cloned.1.call-update
  634.5 127.9 %all-reduce.12.cloned.1.call-done = f32[2048,1024]{1,0:T(8,128)} async-done(((f32[2048,1024]{1,0:T(8,128)}), f32[2048,1024]{1,0:T(8,128)}) %all-reduce.12.cloned.1.call-update) | async-done | bytes 8388624 | tf_op jit(solution)/shard_map/psum | solution.py:9
  762.3 83.5 %conditional.7 = (f32[2048,1024]{1,0:T(8,128)}) conditional(s32[]{:T(128)} %convert_element_type.10, (pred[2048,1]{0,1:T(4,128)(4,1)S(1)}, f32[2048,1024]{1,0:T(8,128)}, f32[2048,1024]{1,0:T(8,128)}, f32[2048,1024]{1,0:T(8,128)}, f32[2048,1024]{1,0:T(8,128)}, /*index=5*/f32[1024,1024]{1,0:T(8,128)}, s32[]{:T(128)}) %tuple.50, ...), branch_computations={%region_10.11_spmd.clone, %region_11.12_spmd} | conditional | flops 51545899008 | bytes 92281352 | solution.py:84
  762.6 31.1 %fusion.18 = f32[2048,1024]{0,1:T(8,128)} fusion(f32[2048,1024]{1,0:T(8,128)} %get-tuple-element.100, f32[1024,1024]{1,0:T(8,128)} %get-tuple-element.101), kind=kOutput, calls=%fused_computation.32 | convolution fusion | flops 25769803776 | bytes 20971520 | tf_op jit(solution)/shard_map/cond/branch_0_fun/dot_general | solution.py:17
  793.8 9.2 %copy.15 = f32[2048,1024]{0,1:T(8,128)} copy(f32[2048,1024]{1,0:T(8,128)} %get-tuple-element.99) | data formatting | bytes 16777216 | tf_op jit(solution)/shard_map
  802.9 33.3 %fusion.15 = f32[2048,1024]{0,1:T(8,128)} fusion(f32[2048,1024]{0,1:T(8,128)} %copy.15, f32[2048,1024]{0,1:T(8,128)} %fusion.18, f32[2048,1024]{1,0:T(8,128)} %get-tuple-element.97, f32[2048,1024]{1,0:T(8,128)} %get-tuple-element.98, s32[]{:T(128)} %get-tuple-element.102, pred[2048]{0:T(1024)(128)(4,1)S(1)} %reduce.1), kind=kOutput, calls=%fused_computation.21 | convolution fusion | flops 25776095232 | bytes 37751296 | tf_op jit(solution)/shard_map/cond/branch_0_fun/dot_general | solution.py:17
  836.3 9.2 %copy.16 = f32[2048,1024]{1,0:T(8,128)} copy(f32[2048,1024]{0,1:T(8,128)} %fusion.15) | data formatting | bytes 16777216 | tf_op jit(solution)/shard_map/cond
  (2 shorter events, 0.1 us)
Async XLA Ops:
  6.5 133.4 %all-reduce.6.cloned.1.call-start = ((), (), s32[]{:S(2)}) async-start(), calls=%async_computation | async-start | bytes 16777216 | tf_op jit(solution)/shard_map/psum | solution.py:9
  11.9 276.8 %all-reduce.8.cloned.1.call-start = ((), (), s32[]{:S(2)}) async-start(), calls=%async_computation.1 | async-start | bytes 8388608 | tf_op jit(solution)/shard_map/psum | solution.py:9
  163.4 466.0 %all-reduce.10.cloned.1.call-start = ((), (), s32[]{:S(2)}) async-start(), calls=%async_computation.2 | async-start | bytes 16777216 | tf_op jit(solution)/shard_map/psum | solution.py:9
  302.8 459.6 %all-reduce.12.cloned.1.call-start = ((), (), s32[]{:S(2)}) async-start(), calls=%async_computation.3 | async-start | bytes 16777216 | tf_op jit(solution)/shard_map/psum | solution.py:9
Sparse Core Ops, SparseCore 0:
  12.0 127.8 all-reduce.5
  163.5 125.1 all-reduce.7
  302.9 326.3 all-reduce.9
  634.6 127.6 all-reduce.11
where the time goes:
time: 858 us; the launch traced here: 853 us
  waiting for transfers between devices  706 us (82%)
  matrix products  64.5 us (8%)
  local copies, waits for them, and re-layouts  40.6 us (5%)
  other arithmetic  18.5 us (2%)
  between operations  13.8 us (2%)
  loops' own time  9.66 us (1%)
    psum x4, waiting for transfers between devices, spread(): return lax.psum(block, axis)  706 us
    dot_general x2, matrix products, matmul_bt(): lax.dot_general(left, right, (((1,), (1,)), ((), ())), precision=lax.Prec...  64.5 us
    another operation x5, local copies, waits for them, and re-layouts  24.8 us
    select_n x4, other arithmetic, spread(): jnp.where(lax.axis_index(axis) == holder, block, jnp.zeros_like(block))  18.4 us
  transfers between devices with their start and end apart: 4, of which 4 were waited for; matrix products, arithmetic and copies ran while one was open for 0% of the time, Pallas kernels for 0%

commit v1 on v0

v1 whole, which is shorter than its diff:
```python
import functools

import jax
import jax.numpy as jnp
from jax import lax
from jax.experimental import pallas as pl
from jax.experimental.pallas import tpu as pltpu
from jax.sharding import PartitionSpec as P

MESH = pl.DeviceIdType.MESH
STEPS = 16


def bits_of(count):
    return max(count.bit_length() - 1, 0)


def ring_pos(index, count):
    if count & (count - 1):
        return index
    parity, place = 0, 0
    for bit in reversed(range(bits_of(count))):
        parity = (parity + (index // 2**bit) % 2) % 2
        place = place + parity * 2**bit
    return place


def ring_at(place, count):
    if count & (count - 1):
        return place
    index = 0
    for bit in range(bits_of(count)):
        index = index + (((place // 2**bit) % 2 + (place // 2 ** (bit + 1)) % 2) % 2) * 2**bit
    return index


def move_kernel(
    rows_n, cols_n, width, half, a_ref, l_ref, rows_ref, top_ref, tile_ref, lower_ref, couple_ref, zs, zr, rs, rr
):
    row, col = lax.axis_index("row"), lax.axis_index("col")
    depth = a_ref.shape[0]
    blocks = depth // width
    chunk = width // 2 // STEPS
    z_steps = blocks * STEPS
    span = depth // z_steps
    place = ring_pos(row, rows_n)
    root = (col * width) // depth
    root_place = ring_pos(root, rows_n)
    offset = (col * width) % depth
    z_next = (col + 1) % cols_n
    z_last = (col + cols_n - 1) % cols_n
    r_next = (ring_at((place + 1) % rows_n, rows_n), ring_at((place + rows_n - 1) % rows_n, rows_n))

    barrier = pltpu.get_barrier_semaphore()
    for other in (z_next, z_last):
        pl.semaphore_signal(barrier, inc=1, device_id=(row, other), device_id_type=MESH)
    for other in r_next:
        pl.semaphore_signal(barrier, inc=1, device_id=(other, col), device_id_type=MESH)
    pl.semaphore_wait(barrier, 4)

    def z_copy(step, source):
        at = step * span
        return pltpu.make_async_remote_copy(
            src_ref=source.at[pl.ds(at, span)],
            dst_ref=rows_ref.at[pl.ds(at, span)],
            send_sem=zs.at[step],
            recv_sem=zr.at[step],
            device_id=(row, z_next),
            device_id_type=MESH,
        )

    z_sends = col != cols_n - 1

    def z_step(step):
        @pl.when(col == 0)
        def _():
            z_copy(step, a_ref).start()

        @pl.when(col != 0)
        def _():
            z_copy(step, rows_ref).wait_recv()

            @pl.when(z_sends)
            def _():
                z_copy(step, rows_ref).start()

    small = half // 2 // STEPS
    items = (
        (couple_ref, small, half // 2, 0),
        (lower_ref, chunk, width // 2, root_place),
        (top_ref, chunk, width // 2, 0),
        (tile_ref, chunk, width // 2, root_place),
    )

    def distance(item, way):
        start = items[item][3]
        return (place - start + rows_n) % rows_n if way == 0 else (start - place + rows_n) % rows_n

    def r_copy(item, way, step, source, shift, columns=None):
        buffer, count, part, _ = items[item]
        at = (2 * step + way) * count
        view = source.at[pl.ds(shift + at, count)] if columns is None else source.at[pl.ds(shift + at, count), columns]
        return pltpu.make_async_remote_copy(
            src_ref=view,
            dst_ref=buffer.at[pl.ds(at, count)],
            send_sem=rs.at[item, way, step],
            recv_sem=rr.at[item, way, step],
            device_id=(r_next[way], col),
            device_id_type=MESH,
        )

    def r_step(item, way, step):
        far = distance(item, way)

        @pl.when(far == 0)
        def _():
            if item == 0:
                r_copy(item, way, step, l_ref, half, pl.ds(0, half)).start()
            elif item == 1:
                r_copy(item, way, step, l_ref, offset).start()
            elif item == 2:
                @pl.when(col == 0)
                def _():
                    r_copy(item, way, step, a_ref, 0).start()

                @pl.when(col != 0)
                def _():
                    r_copy(item, way, step, rows_ref, 0).start()
            else:
                r_copy(item, way, step, rows_ref, offset).start()

        @pl.when(far != 0)
        def _():
            r_copy(item, way, step, items[item][0], 0).wait_recv()

            @pl.when(far != rows_n - 1)
            def _():
                r_copy(item, way, step, items[item][0], 0).start()

    def wanted(item):
        return col != 0 if item in (1, 3) else col >= 0

    first = (0, 0, 0, z_steps - STEPS)

    @pl.loop(0, z_steps + rows_n - 1)
    def _(i):
        @pl.when(i < z_steps)
        def _():
            z_step(i)

        for item in range(4):
            for way in range(2):
                step = i - distance(item, way) - first[item]

                @pl.when(jnp.logical_and(wanted(item), jnp.logical_and(step >= 0, step < STEPS)))
                def _():
                    r_step(item, way, step)

    @pl.loop(0, z_steps)
    def _(i):
        @pl.when(z_sends)
        def _():
            z_copy(i, rows_ref).wait_send()

    @pl.loop(0, STEPS)
    def _(i):
        for item in range(4):
            for way in range(2):
                @pl.when(jnp.logical_and(wanted(item), distance(item, way) != rows_n - 1))
                def _():
                    r_copy(item, way, i, items[item][0], 0).wait_send()


def move(rows_n, cols_n, width, half, a_window, l_panel):
    depth = a_window.shape[0]
    f32 = jnp.float32
    square = jax.ShapeDtypeStruct((width, width), f32)
    z_steps = depth // width * STEPS
    return pl.pallas_call(
        functools.partial(move_kernel, rows_n, cols_n, width, half),
        out_shape=(
            jax.ShapeDtypeStruct((depth, width), f32),
            square,
            square,
            square,
            jax.ShapeDtypeStruct((half, half), f32),
        ),
        in_specs=[pl.BlockSpec(memory_space=pl.ANY)] * 2,
        out_specs=[pl.BlockSpec(memory_space=pl.ANY)] * 5,
        scratch_shapes=[
            pltpu.SemaphoreType.DMA((z_steps,)),
            pltpu.SemaphoreType.DMA((z_steps,)),
            pltpu.SemaphoreType.DMA((4, 2, STEPS)),
            pltpu.SemaphoreType.DMA((4, 2, STEPS)),
        ],
        compiler_params=pltpu.CompilerParams(collective_id=0, has_side_effects=True),
    )(a_window, l_panel)


def dot(left, right, dims=((1,), (0,)), precision=lax.Precision.HIGH):
    return lax.dot_general(left, right, (dims, ((), ())), precision=precision, preferred_element_type=jnp.float32)


def split(value):
    high = value.astype(jnp.bfloat16)
    return high, (value - high.astype(jnp.float32)).astype(jnp.bfloat16)


def three_pass(left, high, low, dims):
    left_high, left_low = split(left)
    total = lax.dot_general(left_high, high, (dims, ((), ())), preferred_element_type=jnp.float32)
    total += lax.dot_general(left_high, low, (dims, ((), ())), preferred_element_type=jnp.float32)
    return total + lax.dot_general(left_low, high, (dims, ((), ())), preferred_element_type=jnp.float32)


def prepare_kernel(
    width, flags, low_own, low_got, tile_own, tile_got, a_ref, moved_ref, top_ref, inv_ref, key_ref, weight_ref, th, tl, ih, il
):
    at = pl.program_id(0)
    count = low_own.shape[0]
    in_panel, first_row, here = flags[0] == 1, flags[1] == 1, flags[2] == 1
    nn, nt = ((1,), (0,)), ((1,), (1,))

    @pl.when(at == 0)
    def _():
        @pl.loop(0, width // 128)
        def _(i):
            rows = pl.ds(i * 128, 128)
            own = jnp.where(in_panel, a_ref[rows], moved_ref[rows])
            th[rows], tl[rows] = split(jnp.where(first_row, own, top_ref[rows]))
            ih[rows], il[rows] = split(inv_ref[rows])

    lower = jnp.where(here, low_own[...], low_got[...])
    tile = jnp.where(here, tile_own[...], tile_got[...])
    inverse = inv_ref[pl.ds(pl.multiple_of(at * count, count), count)]
    scaled = three_pass(lower, ih[...], il[...], nn)
    left = jnp.where(in_panel, inverse, -0.5 * scaled)
    other = jnp.where(in_panel, 0.0, left)
    total = three_pass(left, th[...], tl[...], nt) + three_pass(other, th[...], tl[...], nn)
    weight_ref[...] = jnp.where(in_panel, 0.0, tile) + total
    key_ref[...] = jnp.where(in_panel, -inverse, scaled)


def prepare(flags, a_window, moved, l_panel, top, tile, lower, inverse):
    width = a_window.shape[1]
    count = min(256, width)
    own = pl.BlockSpec((count, width), lambda i, f: (f[3] * (width // count) + i, 0))
    block = pl.BlockSpec((count, width), lambda i, f: (i, 0))
    whole = pl.BlockSpec((width, width), lambda i, f: (0, 0))
    square = jax.ShapeDtypeStruct((width, width), jnp.float32)
    return pl.pallas_call(
        functools.partial(prepare_kernel, width),
        out_shape=(square, square),
        grid_spec=pltpu.PrefetchScalarGridSpec(
            num_scalar_prefetch=1,
            grid=(width // count,),
            in_specs=[own, block, own, block, whole, whole, whole, whole],
            out_specs=[block, block],
            scratch_shapes=[pltpu.VMEM((width, width), jnp.bfloat16)] * 4,
        ),
        compiler_params=pltpu.CompilerParams(
            dimension_semantics=("arbitrary",), vmem_limit_bytes=60 * 1024 * 1024
        ),
    )(flags, l_panel, lower, moved, tile, a_window, moved, top, inverse)


def update_kernel(
    width, flags, a_ref, moved_ref, l_ref, inv_ref, key_ref, weight_ref, out_ref, ih, il, kh, kl, wh, wl
):
    at = pl.program_id(0)
    count = a_ref.shape[0]
    half = width // 2

    @pl.when(at == 0)
    def _():
        for source, high, low in ((inv_ref, ih, il), (key_ref, kh, kl), (weight_ref, wh, wl)):
            @pl.loop(0, width // 128)
            def _(i):
                rows = pl.ds(i * 128, 128)
                high[rows], low[rows] = split(source[rows])

    in_panel = flags[0] == 1
    is_top = jnp.logical_and(flags[1] == 1, at * count < width)
    lower = l_ref[...]
    nn, nt = ((1,), (0,)), ((1,), (1,))
    scaled = jnp.concatenate(
        [
            three_pass(lower, ih[:, :half], il[:, :half], nn),
            three_pass(lower[:, half:], ih[half:, half:], il[half:, half:], nn),
        ],
        1,
    )
    own = inv_ref[pl.ds(pl.multiple_of((at * count) % width, count), count)]
    fill = jnp.where(in_panel, -own, 0.0)
    scaled = jnp.where(is_top, fill, scaled)
    window = a_ref[...]
    left = jnp.where(is_top, 0.0, jnp.where(in_panel, window, moved_ref[...]))
    base = jnp.where(in_panel, 0.0, window)
    total = three_pass(left, kh[...], kl[...], nt)
    out_ref[...] = base - (total + three_pass(scaled, wh[...], wl[...], nt))


def update(flags, a_window, moved, l_panel, inverse, key, weight):
    depth, width = a_window.shape
    count = min(256, width)
    block = pl.BlockSpec((count, width), lambda i, f: (i, 0))
    whole = pl.BlockSpec((width, width), lambda i, f: (0, 0))
    return pl.pallas_call(
        functools.partial(update_kernel, width),
        out_shape=jax.ShapeDtypeStruct((depth, width), jnp.float32),
        grid_spec=pltpu.PrefetchScalarGridSpec(
            num_scalar_prefetch=1,
            grid=(depth // count,),
            in_specs=[block, block, block, whole, whole, whole],
            out_specs=block,
            scratch_shapes=[pltpu.VMEM((width, width), jnp.bfloat16)] * 6,
        ),
        compiler_params=pltpu.CompilerParams(
            dimension_semantics=("arbitrary",), vmem_limit_bytes=60 * 1024 * 1024
        ),
    )(flags, a_window, moved, l_panel, inverse, key, weight)


def body(rows_n, cols_n, a_window, l_panel, l_inverse):
    depth, width = a_window.shape
    half = l_inverse.shape[1]
    row, col = lax.axis_index("row"), lax.axis_index("col")
    root, offset = (col * width) // depth, (col * width) % depth
    first_inv, second_inv = l_inverse[0], l_inverse[1]
    moved, top, tile, lower, couple = move(rows_n, cols_n, width, half, a_window, l_panel)
    in_panel = col == 0
    couple = jnp.where(row == 0, l_panel[half:width, :half], couple)

    full = lax.Precision.HIGHEST
    corner = -dot(second_inv, dot(couple, first_inv, precision=full), precision=full)
    inverse = jnp.concatenate(
        [jnp.concatenate([first_inv, jnp.zeros_like(first_inv)], 1), jnp.concatenate([corner, second_inv], 1)], 0
    )
    flags = jnp.stack([jnp.int32(in_panel), jnp.int32(row == 0), jnp.int32(row == root), offset // width])
    key, weight = prepare(flags, a_window, moved, l_panel, top, tile, lower, inverse)
    return update(flags, a_window, moved, l_panel, inverse, key, weight)


def solution(mesh):
    placed = (P("row", "col"), P("row", None), P())
    return jax.shard_map(
        functools.partial(body, mesh.shape["row"], mesh.shape["col"]),
        mesh=mesh,
        in_specs=placed,
        out_specs=P("row", "col"),
        check_vma=False,
    )
```

time: 858 us -> 312 us (0.36)
  waiting for transfers between devices: 706 us -> 0 us
  Pallas kernels: 0 us -> 300 us
  matrix products: 64.5 us -> 5.38 us
  local copies, waits for them, and re-layouts: 40.6 us -> 2.69 us
  other arithmetic: 18.5 us -> 3.04 us
  between operations: 13.8 us -> 0.05 us
  loops' own time: 9.66 us -> 0 us
    psum x4 -> x0, waiting for transfers between devices: 706 us -> none  [spread(): return lax.psum(block, axis)]
    pallas_call x0 -> x3, Pallas kernels: none -> 300 us  [the longest x1 221 us: move(): pl.pallas_call(functools.partial(move_kernel, rows_n, cols_n, width, half...]
    dot_general x2, matrix products: 64.5 us -> 5.38 us  [dot(): lax.dot_general(left, right, (dims, ((), ())), precision=precision, prefe...]
    another operation x5 -> x0, local copies, waits for them, and re-layouts: 24.8 us -> none
    select_n x4 -> x0, other arithmetic: 18.4 us -> none  [spread(): jnp.where(lax.axis_index(axis) == holder, block, jnp.zeros_like(block))]
    another operation x4 -> x0, loops' own time: 9.66 us -> none  [the longest x1 8.89 us: body(): solved = lax.cond(panel_col, solve_panel, lambda: zeros_wide)]
    cond x1 -> x0, local copies, waits for them, and re-layouts: 9.24 us -> none
  transfers between devices with their start and end apart: 4 -> 0, of which waited for: 4 -> 0; matrix products, arithmetic and copies ran while one was open for 0% -> 0% of each run, Pallas kernels for 0% -> 0%
where the time goes in v1:
time: 312 us; the launch traced here: 311 us
  Pallas kernels  300 us (96%)
  matrix products  5.38 us (2%)
    pallas_call x1, Pallas kernels, move(): pl.pallas_call(functools.partial(move_kernel, rows_n, cols_n, width, half...  221 us
    pallas_call x1, Pallas kernels, update(): pl.pallas_call(functools.partial(update_kernel, width), out_shape=jax.Sha...  47.8 us
    pallas_call x1, Pallas kernels, prepare(): pl.pallas_call(functools.partial(prepare_kernel, width), out_shape=(squar...  31.8 us

profile of v1, /device:TPU:27, one launch (start us, length us, event | category | flops | bytes accessed | tf_op | source)
XLA Modules:
  0.0 311.4 jit_solution(3631999231089828407)
XLA Ops:
  0.0 0.6 pad_add_fusion.flags
  0.6 2.7 slice_bitcast_fusion
  3.3 0.0 copy-start
  3.3 220.6 %shard_map.37 = (f32[2048,1024]{1,0:T(8,128)}, f32[1024,1024]{1,0:T(8,128)}, f32[1024,1024]{1,0:T(8,128)}, f32[1024,1024]{1,0:T(8,128)}, f32[512,512]{1,0:T(8,128)}) custom-call(f32[2048,1024]{1,0:T(8,128)} %a_ref.5, f32[2048,1024]{1,0:T(8,128)} %l_ref.3), custom_call_target="tpu_custom_call" | custom-call | tf_op jit(solution)/shard_map/pallas_call | solution.py:179
  223.9 0.0 copy-start.1
  223.9 0.0 copy-done
  223.9 3.5 %fusion.1 = f32[512,512]{1,0:T(8,128)S(1)} fusion(f32[512,512]{1,0:T(8,128)} %get-tuple-element.13, f32[2048,1024]{1,0:T(8,128)} %l_ref.3, pred[]{:T(512)S(6)} %eq.13, f32[2,512,512]{2,1,0:T(8,128)S(1)} %copy-done), kind=kOutput, calls=%fused_computation.5 | convolution fusion | flops 1610874880 | bytes 4194305 | tf_op jit(solution)/shard_map/dot_general | solution.py:201
  227.4 1.9 fusion
  229.3 0.0 copy-done.1
  229.3 2.4 select_maximum_fusion.inv_ref
  231.8 31.8 %shard_map.38 = (f32[1024,1024]{1,0:T(8,128)}, f32[1024,1024]{1,0:T(8,128)}) custom-call(s32[4]{0:T(128)} %pad_add_fusion.flags, f32[2048,1024]{1,0:T(8,128)} %l_ref.3, f32[1024,1024]{1,0:T(8,128)} %get-tuple-element.14.low_got, f32[2048,1024]{1,0:T(8,128)} %get-tuple-element.12.tile_own.moved_ref, f32[1024,1024]{1,0:T(8,128)} %get-tuple-element.15.tile_got, ...), custom_call_target="tpu_custom_call" | custom-call | tf_op jit(solution)/shard_map/pallas_call | solution.py:251
  263.6 47.8 %shard_map.39 = f32[2048,1024]{1,0:T(8,128)} custom-call(s32[4]{0:T(128)} %pad_add_fusion.flags, f32[2048,1024]{1,0:T(8,128)} %a_ref.5, f32[2048,1024]{1,0:T(8,128)} %get-tuple-element.12.tile_own.moved_ref, f32[2048,1024]{1,0:T(8,128)} %l_ref.3, f32[1024,1024]{1,0:T(8,128)} %select_maximum_fusion.inv_ref, f32[1024,1024]{1,0:T(8,128)} %get-tuple-element.17.key_ref, ...), custom_call_target="tpu_custom_call" | custom-call | tf_op jit(solution)/shard_map/pallas_call | solution.py:308
Async XLA Ops:
  3.3 220.6 %copy-start = (f32[2,512,512]{2,1,0:T(8,128)S(1)}, f32[2,512,512]{2,1,0:T(8,128)}, u32[]{:S(2)}) copy-start(f32[2,512,512]{2,1,0:T(8,128)} %param.5) | copy-start | bytes 6291460
  223.9 5.4 %copy-start.1 = (f32[512,512]{1,0:T(8,128)S(1)}, f32[512,512]{1,0:T(8,128)}, u32[]{:S(2)}) copy-start(f32[512,512]{1,0:T(8,128)} %get-tuple-element.20) | copy-start | bytes 3145732
